TPU v7x, 32 devices: a whole 2x2x4 slice. The times are simulated.
32 devices in a mesh: ctx: 16 (over z, y, x), tp: 2 (over core).
Axes of the slice: x: 2, y: 2, z: 4, core: 2. Of those that a mesh axis runs over, the one named last changes fastest.
Arguments:
- hidden_states: bfloat16 [4096, 8192], P('ctx', 'tp'), may hold values from -6 to 6
- queries: bfloat16 [4096, 4096], P('ctx', 'tp')
- key_matrix: bfloat16 [8192, 1024], P('tp'), may hold values from -0.0625 to 0.0625
- value_matrix: bfloat16 [8192, 1024], P('tp'), may hold values from -0.0625 to 0.0625
- stretch_table: int32 [32], replicated, may hold values from 0 to 31, as said below
Outputs:
- attended: bfloat16 [4096, 4096], P('ctx', 'tp')
Inputs may be any that keep to these rules, and one draw needn't show every extreme that they name: `stretch_table`: a permutation of 0 to 31 in which entries 2 i and 2 i + 1 are two stretches c and 31 - c.
All inputs are finite; a program needn't handle non-finite values.
Results may differ from a plain program's by a relative error of at most 0.007.
The roundings to bfloat16 on the way count: a program that leaves them out, or rounds other values in their place, can miss the bound.
Values may be sent and summed in bfloat16 or wider, within the bound.
A program may use at most 256 MiB of HBM per device.

v0:
```python
import math
import jax
import jax.numpy as jnp
from jax import lax
from jax.sharding import PartitionSpec as P

KEY_VALUE_HEADS = 8
HEAD_SIZE = 128


def stretch_position(stretch_ids, stretch_table):
    listed = jnp.arange(stretch_table.shape[0], dtype=jnp.int32)
    onehot = stretch_ids[:, None] == listed[None, :]
    return jnp.sum(jnp.where(onehot, stretch_table[None, :], 0), axis=1)


def body(hidden_states, queries, key_matrix, value_matrix, stretch_table):
    tokens_dev = hidden_states.shape[0]
    key_tiles = key_matrix.reshape(key_matrix.shape[0], KEY_VALUE_HEADS, HEAD_SIZE)
    value_tiles = value_matrix.reshape(value_matrix.shape[0], KEY_VALUE_HEADS, HEAD_SIZE)
    head_group = KEY_VALUE_HEADS // lax.axis_size("tp")
    key_term = jnp.einsum(
        "tc,chd->htd", hidden_states, key_tiles, preferred_element_type=jnp.float32
    )
    value_term = jnp.einsum(
        "tc,chd->htd", hidden_states, value_tiles, preferred_element_type=jnp.float32
    )
    shares = lax.psum_scatter(
        jnp.stack([key_term, value_term], axis=1), "tp", scatter_dimension=0, tiled=True
    )
    kv_local = shares.astype(jnp.bfloat16).transpose(2, 0, 1, 3)
    stretch = tokens_dev // 2
    ctx_size = lax.axis_size("ctx")
    all_rows = jnp.arange(ctx_size * tokens_dev, dtype=jnp.int32)
    all_places = stretch_position(all_rows // stretch, stretch_table) * stretch + all_rows % stretch
    device = lax.axis_index("ctx")
    query_place = lax.dynamic_slice_in_dim(all_places, device * tokens_dev, tokens_dev, 0)
    query_heads = queries.shape[1] // HEAD_SIZE
    group_ratio = query_heads // head_group
    query_grid = queries.reshape(tokens_dev, head_group, group_ratio, HEAD_SIZE)
    scale = 1.0 / HEAD_SIZE**0.5
    span_queries = (query_grid[:stretch], query_grid[stretch:])
    span_places = (query_place[:stretch], query_place[stretch:])
    span_latest = (jnp.max(span_places[0]), jnp.max(span_places[1]))

    def fresh():
        return (
            jnp.full((head_group, group_ratio, stretch), -1e30, jnp.float32),
            jnp.zeros((head_group, group_ratio, stretch), jnp.float32),
            jnp.zeros((head_group, group_ratio, stretch, HEAD_SIZE), jnp.float32),
        )

    carry = (fresh(), fresh())
    piece = lax.all_gather(kv_local, "ctx", axis=0, tiled=True)
    rows = piece.shape[0]
    width = math.gcd(rows, 1024)
    blocks = rows // width

    def visit(state, index):
        begin = index * width
        block = lax.dynamic_slice_in_dim(piece, begin, width, 0)
        key_place = lax.dynamic_slice_in_dim(all_places, begin, width, 0)
        earliest = jnp.min(key_place)
        key_block = block[:, :, 0]
        value_block = block[:, :, 1]
        updated = []
        for span in range(2):
            span_grid = span_queries[span]
            places = span_places[span]

            def attend(inner, span_grid=span_grid, places=places):
                highs, sums, partial_value = inner
                score = (
                    jnp.einsum(
                        "tgrd,ngd->grtn", span_grid, key_block, preferred_element_type=jnp.float32
                    )
                    * scale
                )
                visible = key_place[None, :] <= places[:, None]
                masked = jnp.where(visible, score, jnp.float32(-1e30))
                new_high = jnp.maximum(highs, jnp.max(masked, axis=-1))
                weight = jnp.where(visible, jnp.exp(masked - new_high[..., None]), jnp.float32(0.0))
                factor = jnp.exp(highs - new_high)
                sums = sums * factor + jnp.sum(weight, axis=-1)
                update = jnp.einsum(
                    "grtn,ngd->grtd",
                    weight.astype(jnp.bfloat16),
                    value_block,
                    preferred_element_type=jnp.float32,
                )
                partial_value = partial_value * factor[..., None] + update
                return (new_high, sums, partial_value)

            def keep_state(inner):
                return inner

            updated.append(lax.cond(earliest <= span_latest[span], attend, keep_state, state[span]))
        return ((updated[0], updated[1]), None)

    carry, _ = lax.scan(visit, carry, jnp.arange(blocks, dtype=jnp.int32))
    output = jnp.concatenate(
        [carry[0][2] / carry[0][1][..., None], carry[1][2] / carry[1][1][..., None]], axis=2
    )
    return (
        output.transpose(2, 0, 1, 3)
        .reshape(tokens_dev, query_heads * HEAD_SIZE)
        .astype(jnp.bfloat16)
    )


def solution(mesh):
    in_specs = (P("ctx", "tp"), P("ctx", "tp"), P("tp", None), P("tp", None), P())
    out_specs = P("ctx", "tp")
    return jax.shard_map(body, mesh=mesh, in_specs=in_specs, out_specs=out_specs, check_vma=False)
```

profile of v0, /device:TPU:5, one launch (start us, length us, event | category | flops | bytes accessed | tf_op | source)
XLA Modules:
  0.0 292.8 jit_solution(8657823326039178736)
XLA Ops:
  6.5 11.7 %copy.48 = bf16[4096,1024]{0,1:T(8,128)(2,1)} copy(bf16[4096,1024]{1,0:T(8,128)(2,1)} %param.13) | data formatting | bytes 16777216 | tf_op jit(solution)/shard_map/reshape | solution.py:19
  18.2 11.3 %copy.49 = bf16[4096,1024]{0,1:T(8,128)(2,1)} copy(bf16[4096,1024]{1,0:T(8,128)(2,1)} %param.14) | data formatting | bytes 16777216 | tf_op jit(solution)/shard_map/reshape | solution.py:20
  29.6 5.9 %fusion.34 = f32[8,1,256,128]{2,3,0,1:T(8,128)S(1)} fusion(bf16[4096,8,128]{0,2,1:T(8,128)(2,1)} %bitcast.116, bf16[256,4096]{1,0:T(8,128)(2,1)S(1)} %copy-done), kind=kOutput, calls=%fused_computation.41 | convolution fusion | flops 2147483648 | bytes 11534336 | tf_op jit(solution)/shard_map/tc,chd->htd/dot_general | solution.py:22
  35.5 2.4 fusion.37
  38.1 9.5 %all-reduce.2 = bf16[8,2,256,128]{2,3,0,1:T(8,128)(2,1)S(1)} all-reduce(f32[8,2,256,128]{2,3,0,1:T(8,128)S(1)} %pad_maximum_fusion), channel_id=2, replica_groups=mesh['ctx'=16,'tp'=2] {'tp'}, use_global_device_ids=true, to_apply=%region_0.0.clone | all-reduce | flops 524288 | bytes 3145728
  49.7 1.3 fusion.50
  54.5 130.6 %all-gather.2.cloned.1.call-done = bf16[4096,4,2,128]{0,3,1,2:T(8,128)(2,1)} async-done(((bf16[256,4,2,128]{0,3,1,2:T(8,128)(2,1)}), bf16[4096,4,2,128]{0,3,1,2:T(8,128)(2,1)}) %all-gather.2.cloned.1.call-update) | async-done | bytes 8388624 | tf_op jit(solution)/shard_map/all_gather | solution.py:54
  185.1 1.1 broadcast.66.clone
  186.2 1.1 broadcast.66
  187.3 94.1 %while.20 = (s32[]{:T(128)}, f32[4,4,128]{2,1,0:T(4,128)S(1)}, f32[4,4,128]{2,1,0:T(4,128)S(1)}, f32[4,4,128,128]{3,2,1,0:T(8,128)}, f32[4,4,128]{2,1,0:T(4,128)...) while((s32[]{:T(128)}, f32[4,4,128]{2,1,0:T(4,128)S(1)}, ...), condition=%wide.region_14.15_spmd, body=%wide.region_4.14_spmd.sunk | while | flops 2203329536 | bytes 88360624 | solution.py:100
  191.5 1.8 constant_dynamic-slice_fusion.3
  194.6 8.7 %conditional.4 = ((f32[4,4,128]{2,1,0:T(4,128)S(1)}, f32[4,4,128]{2,1,0:T(4,128)S(1)}, f32[4,4,128,128]{3,2,1,0:T(8,128)})) conditional(s32[]{:T(128)} %convert_element_type.38, (f32[4,4,128]{2,1,0:T(4,128)S(1)}, f32[4,4,128]{2,1,0:T(4,128)S(1)}, f32[4,4,128,128]{3,2,1,0:T(8,128)}) %tuple.57, (s32[1024]{0:T(1024)S(1)}, s32[128]{0:T(128)S(1)}, ...), branch_computations={%region_6.6_spmd, %region_7.9_spmd} | conditional | flops 1101664256 | bytes 38933080 | solution.py:97
  194.9 2.5 fusion
  197.3 2.0 fusion.2
  199.4 2.9 %fusion.6 = f32[4,4,128,128]{3,2,1,0:T(8,128)S(1)} fusion(f32[4,1024,128,4]{2,1,3,0:T(8,128)S(1)} %get-tuple-element.265, f32[4,4,128]{2,1,0:T(4,128)S(1)} %max.4, pred[128,1024]{0,1:T(8,128)(4,1)S(1)} %broadcast_compare_fusion, bf16[1024,4,128]{2,0,1:T(8,128)(2,1)S(1)} %get-tuple-element.120, f32[4,4,128,128]{3,2,1,0:T(8,128)S(1)} %copy-done.5, ...), kind=kOutput, calls=%fused_computation.7 | convolution fusion | flops 547880960 | bytes 11681792 | tf_op jit(solution)/shard_map/while/body/eval_jaxpr/cond/branch_1_fun/grtn,ngd->grtd/dot_general | solution.py:85
  203.3 7.6 %conditional.5 = ((f32[4,4,128]{2,1,0:T(4,128)S(1)}, f32[4,4,128]{2,1,0:T(4,128)S(1)}, f32[4,4,128,128]{3,2,1,0:T(8,128)})) conditional(s32[]{:T(128)} %convert_element_type.39, (f32[4,4,128]{2,1,0:T(4,128)S(1)}, f32[4,4,128]{2,1,0:T(4,128)S(1)}, f32[4,4,128,128]{3,2,1,0:T(8,128)}) %tuple.59, (s32[1024]{0:T(1024)S(1)}, s32[128]{0:T(128)S(1)}, ...), branch_computations={%region_10.10_spmd, %region_11.13_spmd} | conditional | flops 1101664256 | bytes 38933080 | solution.py:97
  203.5 1.3 fusion.15
  204.8 2.0 fusion.17
  206.9 2.9 %fusion.21 = f32[4,4,128,128]{3,2,1,0:T(8,128)S(1)} fusion(f32[4,1024,128,4]{2,1,3,0:T(8,128)S(1)} %get-tuple-element.267, f32[4,4,128]{2,1,0:T(4,128)S(1)} %max.5, pred[128,1024]{0,1:T(8,128)(4,1)S(1)} %broadcast_compare_fusion.1, bf16[1024,4,128]{2,0,1:T(8,128)(2,1)S(1)} %get-tuple-element.128, f32[4,4,128,128]{3,2,1,0:T(8,128)S(1)} %copy-done.3, ...), kind=kOutput, calls=%fused_computation.24 | convolution fusion | flops 547880960 | bytes 11681792 | tf_op jit(solution)/shard_map/while/body/eval_jaxpr/cond/branch_1_fun/grtn,ngd->grtd/dot_general | solution.py:85
  215.0 1.8 constant_dynamic-slice_fusion.3
  218.1 8.7 %conditional.4 = ((f32[4,4,128]{2,1,0:T(4,128)S(1)}, f32[4,4,128]{2,1,0:T(4,128)S(1)}, f32[4,4,128,128]{3,2,1,0:T(8,128)})) conditional(s32[]{:T(128)} %convert_element_type.38, (f32[4,4,128]{2,1,0:T(4,128)S(1)}, f32[4,4,128]{2,1,0:T(4,128)S(1)}, f32[4,4,128,128]{3,2,1,0:T(8,128)}) %tuple.57, (s32[1024]{0:T(1024)S(1)}, s32[128]{0:T(128)S(1)}, ...), branch_computations={%region_6.6_spmd, %region_7.9_spmd} | conditional | flops 1101664256 | bytes 38933080 | solution.py:97
  218.4 2.5 fusion
  220.9 2.0 fusion.2
  222.9 2.9 %fusion.6 = f32[4,4,128,128]{3,2,1,0:T(8,128)S(1)} fusion(f32[4,1024,128,4]{2,1,3,0:T(8,128)S(1)} %get-tuple-element.265, f32[4,4,128]{2,1,0:T(4,128)S(1)} %max.4, pred[128,1024]{0,1:T(8,128)(4,1)S(1)} %broadcast_compare_fusion, bf16[1024,4,128]{2,0,1:T(8,128)(2,1)S(1)} %get-tuple-element.120, f32[4,4,128,128]{3,2,1,0:T(8,128)S(1)} %copy-done.5, ...), kind=kOutput, calls=%fused_computation.7 | convolution fusion | flops 547880960 | bytes 11681792 | tf_op jit(solution)/shard_map/while/body/eval_jaxpr/cond/branch_1_fun/grtn,ngd->grtd/dot_general | solution.py:85
  226.8 7.6 %conditional.5 = ((f32[4,4,128]{2,1,0:T(4,128)S(1)}, f32[4,4,128]{2,1,0:T(4,128)S(1)}, f32[4,4,128,128]{3,2,1,0:T(8,128)})) conditional(s32[]{:T(128)} %convert_element_type.39, (f32[4,4,128]{2,1,0:T(4,128)S(1)}, f32[4,4,128]{2,1,0:T(4,128)S(1)}, f32[4,4,128,128]{3,2,1,0:T(8,128)}) %tuple.59, (s32[1024]{0:T(1024)S(1)}, s32[128]{0:T(128)S(1)}, ...), branch_computations={%region_10.10_spmd, %region_11.13_spmd} | conditional | flops 1101664256 | bytes 38933080 | solution.py:97
  227.0 1.3 fusion.15
  228.4 2.0 fusion.17
  230.4 2.9 %fusion.21 = f32[4,4,128,128]{3,2,1,0:T(8,128)S(1)} fusion(f32[4,1024,128,4]{2,1,3,0:T(8,128)S(1)} %get-tuple-element.267, f32[4,4,128]{2,1,0:T(4,128)S(1)} %max.5, pred[128,1024]{0,1:T(8,128)(4,1)S(1)} %broadcast_compare_fusion.1, bf16[1024,4,128]{2,0,1:T(8,128)(2,1)S(1)} %get-tuple-element.128, f32[4,4,128,128]{3,2,1,0:T(8,128)S(1)} %copy-done.3, ...), kind=kOutput, calls=%fused_computation.24 | convolution fusion | flops 547880960 | bytes 11681792 | tf_op jit(solution)/shard_map/while/body/eval_jaxpr/cond/branch_1_fun/grtn,ngd->grtd/dot_general | solution.py:85
  238.5 1.8 constant_dynamic-slice_fusion.3
  241.7 8.7 %conditional.4 = ((f32[4,4,128]{2,1,0:T(4,128)S(1)}, f32[4,4,128]{2,1,0:T(4,128)S(1)}, f32[4,4,128,128]{3,2,1,0:T(8,128)})) conditional(s32[]{:T(128)} %convert_element_type.38, (f32[4,4,128]{2,1,0:T(4,128)S(1)}, f32[4,4,128]{2,1,0:T(4,128)S(1)}, f32[4,4,128,128]{3,2,1,0:T(8,128)}) %tuple.57, (s32[1024]{0:T(1024)S(1)}, s32[128]{0:T(128)S(1)}, ...), branch_computations={%region_6.6_spmd, %region_7.9_spmd} | conditional | flops 1101664256 | bytes 38933080 | solution.py:97
  241.9 2.5 fusion
  244.4 2.0 fusion.2
  246.4 2.9 %fusion.6 = f32[4,4,128,128]{3,2,1,0:T(8,128)S(1)} fusion(f32[4,1024,128,4]{2,1,3,0:T(8,128)S(1)} %get-tuple-element.265, f32[4,4,128]{2,1,0:T(4,128)S(1)} %max.4, pred[128,1024]{0,1:T(8,128)(4,1)S(1)} %broadcast_compare_fusion, bf16[1024,4,128]{2,0,1:T(8,128)(2,1)S(1)} %get-tuple-element.120, f32[4,4,128,128]{3,2,1,0:T(8,128)S(1)} %copy-done.5, ...), kind=kOutput, calls=%fused_computation.7 | convolution fusion | flops 547880960 | bytes 11681792 | tf_op jit(solution)/shard_map/while/body/eval_jaxpr/cond/branch_1_fun/grtn,ngd->grtd/dot_general | solution.py:85
  250.3 7.6 %conditional.5 = ((f32[4,4,128]{2,1,0:T(4,128)S(1)}, f32[4,4,128]{2,1,0:T(4,128)S(1)}, f32[4,4,128,128]{3,2,1,0:T(8,128)})) conditional(s32[]{:T(128)} %convert_element_type.39, (f32[4,4,128]{2,1,0:T(4,128)S(1)}, f32[4,4,128]{2,1,0:T(4,128)S(1)}, f32[4,4,128,128]{3,2,1,0:T(8,128)}) %tuple.59, (s32[1024]{0:T(1024)S(1)}, s32[128]{0:T(128)S(1)}, ...), branch_computations={%region_10.10_spmd, %region_11.13_spmd} | conditional | flops 1101664256 | bytes 38933080 | solution.py:97
  250.6 1.3 fusion.15
  251.9 2.0 fusion.17
  253.9 2.9 %fusion.21 = f32[4,4,128,128]{3,2,1,0:T(8,128)S(1)} fusion(f32[4,1024,128,4]{2,1,3,0:T(8,128)S(1)} %get-tuple-element.267, f32[4,4,128]{2,1,0:T(4,128)S(1)} %max.5, pred[128,1024]{0,1:T(8,128)(4,1)S(1)} %broadcast_compare_fusion.1, bf16[1024,4,128]{2,0,1:T(8,128)(2,1)S(1)} %get-tuple-element.128, f32[4,4,128,128]{3,2,1,0:T(8,128)S(1)} %copy-done.3, ...), kind=kOutput, calls=%fused_computation.24 | convolution fusion | flops 547880960 | bytes 11681792 | tf_op jit(solution)/shard_map/while/body/eval_jaxpr/cond/branch_1_fun/grtn,ngd->grtd/dot_general | solution.py:85
  262.0 1.8 constant_dynamic-slice_fusion.3
  265.2 8.7 %conditional.4 = ((f32[4,4,128]{2,1,0:T(4,128)S(1)}, f32[4,4,128]{2,1,0:T(4,128)S(1)}, f32[4,4,128,128]{3,2,1,0:T(8,128)})) conditional(s32[]{:T(128)} %convert_element_type.38, (f32[4,4,128]{2,1,0:T(4,128)S(1)}, f32[4,4,128]{2,1,0:T(4,128)S(1)}, f32[4,4,128,128]{3,2,1,0:T(8,128)}) %tuple.57, (s32[1024]{0:T(1024)S(1)}, s32[128]{0:T(128)S(1)}, ...), branch_computations={%region_6.6_spmd, %region_7.9_spmd} | conditional | flops 1101664256 | bytes 38933080 | solution.py:97
  265.4 2.5 fusion
  267.9 2.0 fusion.2
  269.9 2.9 %fusion.6 = f32[4,4,128,128]{3,2,1,0:T(8,128)S(1)} fusion(f32[4,1024,128,4]{2,1,3,0:T(8,128)S(1)} %get-tuple-element.265, f32[4,4,128]{2,1,0:T(4,128)S(1)} %max.4, pred[128,1024]{0,1:T(8,128)(4,1)S(1)} %broadcast_compare_fusion, bf16[1024,4,128]{2,0,1:T(8,128)(2,1)S(1)} %get-tuple-element.120, f32[4,4,128,128]{3,2,1,0:T(8,128)S(1)} %copy-done.5, ...), kind=kOutput, calls=%fused_computation.7 | convolution fusion | flops 547880960 | bytes 11681792 | tf_op jit(solution)/shard_map/while/body/eval_jaxpr/cond/branch_1_fun/grtn,ngd->grtd/dot_general | solution.py:85
  273.9 7.6 %conditional.5 = ((f32[4,4,128]{2,1,0:T(4,128)S(1)}, f32[4,4,128]{2,1,0:T(4,128)S(1)}, f32[4,4,128,128]{3,2,1,0:T(8,128)})) conditional(s32[]{:T(128)} %convert_element_type.39, (f32[4,4,128]{2,1,0:T(4,128)S(1)}, f32[4,4,128]{2,1,0:T(4,128)S(1)}, f32[4,4,128,128]{3,2,1,0:T(8,128)}) %tuple.59, (s32[1024]{0:T(1024)S(1)}, s32[128]{0:T(128)S(1)}, ...), branch_computations={%region_10.10_spmd, %region_11.13_spmd} | conditional | flops 1101664256 | bytes 38933080 | solution.py:97
  274.1 1.3 fusion.15
  275.4 2.0 fusion.17
  277.4 2.9 %fusion.21 = f32[4,4,128,128]{3,2,1,0:T(8,128)S(1)} fusion(f32[4,1024,128,4]{2,1,3,0:T(8,128)S(1)} %get-tuple-element.267, f32[4,4,128]{2,1,0:T(4,128)S(1)} %max.5, pred[128,1024]{0,1:T(8,128)(4,1)S(1)} %broadcast_compare_fusion.1, bf16[1024,4,128]{2,0,1:T(8,128)(2,1)S(1)} %get-tuple-element.128, f32[4,4,128,128]{3,2,1,0:T(8,128)S(1)} %copy-done.3, ...), kind=kOutput, calls=%fused_computation.24 | convolution fusion | flops 547880960 | bytes 11681792 | tf_op jit(solution)/shard_map/while/body/eval_jaxpr/cond/branch_1_fun/grtn,ngd->grtd/dot_general | solution.py:85
  281.4 2.1 divide_convert_fusion
  284.4 1.6 convert_element_type.24
  (122 shorter events, 25.9 us)
Async XLA Ops:
  6.5 23.0 %copy-start = (bf16[256,4096]{1,0:T(8,128)(2,1)S(1)}, bf16[256,4096]{1,0:T(8,128)(2,1)}, u32[]{:S(2)}) copy-start(bf16[256,4096]{1,0:T(8,128)(2,1)} %param.11) | copy-start | bytes 6291460
  6.5 178.5 %all-gather.2.cloned.1.call-start = ((), (), s32[]{:S(2)}) async-start(), calls=%async_computation | async-start | bytes 8912896 | tf_op jit(solution)/shard_map/all_gather | solution.py:54
  29.5 5.9 %slice-start = ((s8[8388608]{0:T(1024)(128)(4,1)}), s8[4194304]{0:T(1024)(128)(4,1)S(1)}, s32[]{:S(2)}) async-start(s8[8388608]{0:T(1024)(128)(4,1)} %bitcast.113), calls=%async_computation.1 | async-start | bytes 8388608
  29.5 5.9 %slice-start.1 = ((s8[8388608]{0:T(1024)(128)(4,1)}), s8[4194304]{0:T(1024)(128)(4,1)S(1)}, s32[]{:S(2)}) async-start(s8[8388608]{0:T(1024)(128)(4,1)} %bitcast.113), calls=%async_computation.2 | async-start | bytes 8388608
  35.5 12.1 %copy-start.8 = (u32[32]{0:T(128)S(1)}, u32[32]{0:T(128)}, u32[]{:S(2)}) copy-start(u32[32]{0:T(128)} %constant.81) | copy-start | bytes 388
  37.9 15.7 %copy-start.7 = (s32[32]{0:T(128)S(1)}, s32[32]{0:T(128)}, u32[]{:S(2)}) copy-start(s32[32]{0:T(128)} %param.15) | copy-start | bytes 388
  194.6 8.7 %copy-start.2 = (bf16[128,4,4,128]{3,0,2,1:T(8,128)(2,1)S(1)}, bf16[128,4,4,128]{3,0,2,1:T(8,128)(2,1)}, u32[]{:S(2)}) copy-start(bf16[128,4,4,128]{3,0,2,1:T(8,128)(2,1)} %get-tuple-element.466) | copy-start | bytes 1572868 | tf_op jit(solution)/shard_map/while
  194.9 4.5 %copy-start.5 = (f32[4,4,128,128]{3,2,1,0:T(8,128)S(1)}, f32[4,4,128,128]{3,2,1,0:T(8,128)}, u32[]{:S(2)}) copy-start(f32[4,4,128,128]{3,2,1,0:T(8,128)} %get-tuple-element.119) | copy-start | bytes 3145732 | tf_op jit(solution)/shard_map/while/body/eval_jaxpr/cond
  202.3 1.0 copy-start.6
  203.5 3.4 %copy-start.3 = (f32[4,4,128,128]{3,2,1,0:T(8,128)S(1)}, f32[4,4,128,128]{3,2,1,0:T(8,128)}, u32[]{:S(2)}) copy-start(f32[4,4,128,128]{3,2,1,0:T(8,128)} %get-tuple-element.127) | copy-start | bytes 3145732 | tf_op jit(solution)/shard_map/while/body/eval_jaxpr/cond
  209.8 1.0 copy-start.4
  218.1 8.7 %copy-start.2 = (bf16[128,4,4,128]{3,0,2,1:T(8,128)(2,1)S(1)}, bf16[128,4,4,128]{3,0,2,1:T(8,128)(2,1)}, u32[]{:S(2)}) copy-start(bf16[128,4,4,128]{3,0,2,1:T(8,128)(2,1)} %get-tuple-element.466) | copy-start | bytes 1572868 | tf_op jit(solution)/shard_map/while
  218.4 4.5 %copy-start.5 = (f32[4,4,128,128]{3,2,1,0:T(8,128)S(1)}, f32[4,4,128,128]{3,2,1,0:T(8,128)}, u32[]{:S(2)}) copy-start(f32[4,4,128,128]{3,2,1,0:T(8,128)} %get-tuple-element.119) | copy-start | bytes 3145732 | tf_op jit(solution)/shard_map/while/body/eval_jaxpr/cond
  225.8 1.0 copy-start.6
  227.0 3.4 %copy-start.3 = (f32[4,4,128,128]{3,2,1,0:T(8,128)S(1)}, f32[4,4,128,128]{3,2,1,0:T(8,128)}, u32[]{:S(2)}) copy-start(f32[4,4,128,128]{3,2,1,0:T(8,128)} %get-tuple-element.127) | copy-start | bytes 3145732 | tf_op jit(solution)/shard_map/while/body/eval_jaxpr/cond
  233.3 1.0 copy-start.4
  241.7 8.7 %copy-start.2 = (bf16[128,4,4,128]{3,0,2,1:T(8,128)(2,1)S(1)}, bf16[128,4,4,128]{3,0,2,1:T(8,128)(2,1)}, u32[]{:S(2)}) copy-start(bf16[128,4,4,128]{3,0,2,1:T(8,128)(2,1)} %get-tuple-element.466) | copy-start | bytes 1572868 | tf_op jit(solution)/shard_map/while
  241.9 4.5 %copy-start.5 = (f32[4,4,128,128]{3,2,1,0:T(8,128)S(1)}, f32[4,4,128,128]{3,2,1,0:T(8,128)}, u32[]{:S(2)}) copy-start(f32[4,4,128,128]{3,2,1,0:T(8,128)} %get-tuple-element.119) | copy-start | bytes 3145732 | tf_op jit(solution)/shard_map/while/body/eval_jaxpr/cond
  249.4 1.0 copy-start.6
  250.5 3.4 %copy-start.3 = (f32[4,4,128,128]{3,2,1,0:T(8,128)S(1)}, f32[4,4,128,128]{3,2,1,0:T(8,128)}, u32[]{:S(2)}) copy-start(f32[4,4,128,128]{3,2,1,0:T(8,128)} %get-tuple-element.127) | copy-start | bytes 3145732 | tf_op jit(solution)/shard_map/while/body/eval_jaxpr/cond
  256.9 1.0 copy-start.4
  265.2 8.7 %copy-start.2 = (bf16[128,4,4,128]{3,0,2,1:T(8,128)(2,1)S(1)}, bf16[128,4,4,128]{3,0,2,1:T(8,128)(2,1)}, u32[]{:S(2)}) copy-start(bf16[128,4,4,128]{3,0,2,1:T(8,128)(2,1)} %get-tuple-element.466) | copy-start | bytes 1572868 | tf_op jit(solution)/shard_map/while
  265.4 4.5 %copy-start.5 = (f32[4,4,128,128]{3,2,1,0:T(8,128)S(1)}, f32[4,4,128,128]{3,2,1,0:T(8,128)}, u32[]{:S(2)}) copy-start(f32[4,4,128,128]{3,2,1,0:T(8,128)} %get-tuple-element.119) | copy-start | bytes 3145732 | tf_op jit(solution)/shard_map/while/body/eval_jaxpr/cond
  272.9 1.0 copy-start.6
  274.1 3.4 %copy-start.3 = (f32[4,4,128,128]{3,2,1,0:T(8,128)S(1)}, f32[4,4,128,128]{3,2,1,0:T(8,128)}, u32[]{:S(2)}) copy-start(f32[4,4,128,128]{3,2,1,0:T(8,128)} %get-tuple-element.127) | copy-start | bytes 3145732 | tf_op jit(solution)/shard_map/while/body/eval_jaxpr/cond
  280.4 1.0 copy-start.4
  281.4 4.6 %copy-start.1 = (bf16[256,4096]{1,0:T(8,128)(2,1)S(1)}, bf16[256,4096]{1,0:T(8,128)(2,1)}, u32[]{:S(2)}) copy-start(bf16[256,4096]{1,0:T(8,128)(2,1)} %param.11) | copy-start | bytes 6291460
Sparse Core Ops, SparseCore 0:
  49.8 135.2 all-gather.1
where the time goes:
time: 294 us; the launch traced here: 293 us
  waiting for transfers between devices  131 us (45%)
  local copies, waits for them, and re-layouts  55.9 us (19%)
  matrix products  46.7 us (16%)
  other arithmetic  23.3 us (8%)
  between operations  14.2 us (5%)
  loops' own time  12.5 us (4%)
  blocking collectives  9.51 us (3%)
    all_gather x1, waiting for transfers between devices, body(): piece = lax.all_gather(kv_local, 'ctx', axis=0, tiled=True)  131 us
    dot_general x8, matrix products, attend(): jnp.einsum('grtn,ngd->grtd', weight.astype(jnp.bfloat16), value_block, pr...  23.4 us
    reduce_sum x8, other arithmetic, attend(): sums = sums * factor + jnp.sum(weight, axis=-1)  16 us
    dot_general x8, matrix products, attend(): jnp.einsum('tgrd,ngd->grtn', span_grid, key_block, preferred_element_type...  15 us
    another operation x1, loops' own time, body(): carry, _ = lax.scan(visit, carry, jnp.arange(blocks, dtype=jnp.int32))  11.9 us
    reshape x1, local copies, waits for them, and re-layouts, body(): key_matrix.reshape(key_matrix.shape[0], KEY_VALUE_HEADS, HEAD_SIZE)  11.7 us
    reshape x1, local copies, waits for them, and re-layouts, body(): value_matrix.reshape(value_matrix.shape[0], KEY_VALUE_HEADS, HEAD_SIZE)  11.3 us
    unnamed x1, blocking collectives  9.51 us
  transfers between devices with their start and end apart: 1, of which 1 were waited for; matrix products, arithmetic and copies ran while one was open for 2% of the time, Pallas kernels for 0%

commit v1 on v0

--- a/solution.py
+++ b/solution.py
@@ -6,6 +6,18 @@
 
 KEY_VALUE_HEADS = 8
 HEAD_SIZE = 128
+
+
+def column_try_all(mine_x, link_axis):
+    n_blocks = lax.axis_size(link_axis)
+    shelf = [(dd, (dd + 1) % n_blocks) for dd in range(n_blocks)]
+    t_next = [None] * n_blocks
+    t_next[n_blocks - 1] = mine_x
+    for dev in range(n_blocks - 2, -1, -1):
+        t_next[dev] = lax.ppermute(t_next[dev + 1], link_axis, perm=shelf)
+    v_next = jnp.concatenate(t_next, axis=0)
+    x_new = (lax.axis_index(link_axis) + 1) * mine_x.shape[0]
+    return jnp.roll(v_next, x_new, axis=0)
 
 
 def stretch_position(stretch_ids, stretch_table):
@@ -51,7 +63,7 @@
         )
 
     carry = (fresh(), fresh())
-    piece = lax.all_gather(kv_local, "ctx", axis=0, tiled=True)
+    piece = column_try_all(kv_local, "ctx")
     rows = piece.shape[0]
     width = math.gcd(rows, 1024)
     blocks = rows // width

time: 294 us -> 430 us (1.46)
  the two profiles are of different devices: /device:TPU:5 before, /device:TPU:30 now
where the time goes in v1:
time: 430 us; the launch traced here: 428 us
  waiting for transfers between devices  131 us (30%)
  local copies, waits for them, and re-layouts  116 us (27%)
  starting transfers between devices  83 us (19%)
  matrix products  50.2 us (12%)
  other arithmetic  23.8 us (6%)
  loops' own time  13.6 us (3%)
  blocking collectives  8.98 us (2%)
    ppermute x15, waiting for transfers between devices, column_try_all(): t_next[dev] = lax.ppermute(t_next[dev + 1], link_axis, perm=shelf)  131 us
    ppermute x15, starting transfers between devices, column_try_all(): t_next[dev] = lax.ppermute(t_next[dev + 1], link_axis, perm=shelf)  83 us
    unnamed x70, local copies, waits for them, and re-layouts  50.6 us
    dot_general x8, matrix products, attend(): jnp.einsum('grtn,ngd->grtd', weight.astype(jnp.bfloat16), value_block, pr...  23.4 us
    reduce_sum x8, other arithmetic, attend(): sums = sums * factor + jnp.sum(weight, axis=-1)  16 us
    dot_general x8, matrix products, attend(): jnp.einsum('tgrd,ngd->grtn', span_grid, key_block, preferred_element_type...  15.3 us
    another operation x1, loops' own time, body(): carry, _ = lax.scan(visit, carry, jnp.arange(blocks, dtype=jnp.int32))  12.9 us
    reshape x1, local copies, waits for them, and re-layouts, body(): key_matrix.reshape(key_matrix.shape[0], KEY_VALUE_HEADS, HEAD_SIZE)  11.5 us
  transfers between devices with their start and end apart: 15, of which 15 were waited for; matrix products, arithmetic and copies ran while one was open for 3% of the time, Pallas kernels for 0%

profile of v1, /device:TPU:30, one launch (start us, length us, event | category | flops | bytes accessed | tf_op | source)
XLA Modules:
  0.0 427.8 jit_solution(15971153695580275489)
XLA Ops:
  0.0 11.5 %copy.48 = bf16[4096,1024]{0,1:T(8,128)(2,1)} copy(bf16[4096,1024]{1,0:T(8,128)(2,1)} %param.13) | data formatting | bytes 16777216 | tf_op jit(solution)/shard_map/reshape | solution.py:31
  11.5 11.2 %copy.49 = bf16[4096,1024]{0,1:T(8,128)(2,1)} copy(bf16[4096,1024]{1,0:T(8,128)(2,1)} %param.14) | data formatting | bytes 16777216 | tf_op jit(solution)/shard_map/reshape | solution.py:32
  22.7 5.8 %fusion.34 = f32[8,1,256,128]{2,3,0,1:T(8,128)S(1)} fusion(bf16[4096,8,128]{0,2,1:T(8,128)(2,1)} %bitcast.118, bf16[256,4096]{1,0:T(8,128)(2,1)S(1)} %copy-done), kind=kOutput, calls=%fused_computation.41 | convolution fusion | flops 2147483648 | bytes 11534336 | tf_op jit(solution)/shard_map/tc,chd->htd/dot_general | solution.py:34
  28.5 5.8 %fusion.37 = f32[8,1,256,128]{2,3,0,1:T(8,128)S(1)} fusion(bf16[4096,8,128]{0,2,1:T(8,128)(2,1)} %bitcast.117, bf16[256,4096]{1,0:T(8,128)(2,1)S(1)} %copy-done), kind=kOutput, calls=%fused_computation.42 | convolution fusion | flops 2147483648 | bytes 11534336 | tf_op jit(solution)/shard_map/tc,chd->htd/dot_general | solution.py:37
  34.5 9.0 %all-reduce.2 = bf16[8,2,256,128]{2,3,0,1:T(8,128)(2,1)S(1)} all-reduce(f32[8,2,256,128]{2,3,0,1:T(8,128)S(1)} %pad_maximum_fusion), channel_id=2, replica_groups=mesh['ctx'=16,'tp'=2] {'tp'}, use_global_device_ids=true, to_apply=%region_0.0.clone | all-reduce | flops 524288 | bytes 3145728
  44.8 14.2 %collective-permute-done = bf16[256,4,2,128]{0,3,1,2:T(8,128)(2,1)S(1)} collective-permute-done((bf16[256,4,2,128]{0,3,1,2:T(8,128)(2,1)S(1)}, bf16[256,4,2,128]{0,3,1,2:T(8,128)(2,1)S(1)}, u32[]{:S(2)}, u32[]{:S(2)}) %collective-permute-start) | collective-permute-done | bytes 524320 | tf_op jit(solution)/shard_map/ppermute | solution.py:17
  59.0 3.9 collective-permute-start.1
  62.9 11.1 %collective-permute-done.1 = bf16[256,4,2,128]{0,3,1,2:T(8,128)(2,1)S(1)} collective-permute-done((bf16[256,4,2,128]{0,3,1,2:T(8,128)(2,1)S(1)}, bf16[256,4,2,128]{0,3,1,2:T(8,128)(2,1)S(1)}, u32[]{:S(2)}, u32[]{:S(2)}) %collective-permute-start.1) | collective-permute-done | bytes 524320 | tf_op jit(solution)/shard_map/ppermute | solution.py:17
  74.0 6.1 %collective-permute-start.2 = (bf16[256,4,2,128]{0,3,1,2:T(8,128)(2,1)S(1)}, bf16[256,4,2,128]{0,3,1,2:T(8,128)(2,1)S(1)}, u32[]{:S(2)}, u32[]{:S(2)}) collective-permute-start(bf16[256,4,2,128]{0,3,1,2:T(8,128)(2,1)S(1)} %collective-permute-done.1), channel_id=1, source_target_pairs={{0,2},{2,4},{4,6},{6,8},{8,10},{10,12},{12,14},{14,16},{16,18},{18... | collective-permute-start | bytes 1572872 | tf_op jit(solution)/shard_map/ppermute | solution.py:17
  80.1 10.3 %collective-permute-done.2 = bf16[256,4,2,128]{0,3,1,2:T(8,128)(2,1)S(1)} collective-permute-done((bf16[256,4,2,128]{0,3,1,2:T(8,128)(2,1)S(1)}, bf16[256,4,2,128]{0,3,1,2:T(8,128)(2,1)S(1)}, u32[]{:S(2)}, u32[]{:S(2)}) %collective-permute-start.2) | collective-permute-done | bytes 524320 | tf_op jit(solution)/shard_map/ppermute | solution.py:17
  90.4 6.1 %collective-permute-start.3 = (bf16[256,4,2,128]{0,3,1,2:T(8,128)(2,1)S(1)}, bf16[256,4,2,128]{0,3,1,2:T(8,128)(2,1)S(1)}, u32[]{:S(2)}, u32[]{:S(2)}) collective-permute-start(bf16[256,4,2,128]{0,3,1,2:T(8,128)(2,1)S(1)} %collective-permute-done.2), channel_id=1, source_target_pairs={{0,2},{2,4},{4,6},{6,8},{8,10},{10,12},{12,14},{14,16},{16,18},{18... | collective-permute-start | bytes 1572872 | tf_op jit(solution)/shard_map/ppermute | solution.py:17
  96.5 9.4 %collective-permute-done.3 = bf16[256,4,2,128]{0,3,1,2:T(8,128)(2,1)S(1)} collective-permute-done((bf16[256,4,2,128]{0,3,1,2:T(8,128)(2,1)S(1)}, bf16[256,4,2,128]{0,3,1,2:T(8,128)(2,1)S(1)}, u32[]{:S(2)}, u32[]{:S(2)}) %collective-permute-start.3) | collective-permute-done | bytes 524320 | tf_op jit(solution)/shard_map/ppermute | solution.py:17
  105.9 6.1 %collective-permute-start.4 = (bf16[256,4,2,128]{0,3,1,2:T(8,128)(2,1)S(1)}, bf16[256,4,2,128]{0,3,1,2:T(8,128)(2,1)S(1)}, u32[]{:S(2)}, u32[]{:S(2)}) collective-permute-start(bf16[256,4,2,128]{0,3,1,2:T(8,128)(2,1)S(1)} %collective-permute-done.3), channel_id=1, source_target_pairs={{0,2},{2,4},{4,6},{6,8},{8,10},{10,12},{12,14},{14,16},{16,18},{18... | collective-permute-start | bytes 1572872 | tf_op jit(solution)/shard_map/ppermute | solution.py:17
  112.0 8.6 %collective-permute-done.4 = bf16[256,4,2,128]{0,3,1,2:T(8,128)(2,1)S(1)} collective-permute-done((bf16[256,4,2,128]{0,3,1,2:T(8,128)(2,1)S(1)}, bf16[256,4,2,128]{0,3,1,2:T(8,128)(2,1)S(1)}, u32[]{:S(2)}, u32[]{:S(2)}) %collective-permute-start.4) | collective-permute-done | bytes 524320 | tf_op jit(solution)/shard_map/ppermute | solution.py:17
  121.3 6.1 %collective-permute-start.5 = (bf16[256,4,2,128]{0,3,1,2:T(8,128)(2,1)S(1)}, bf16[256,4,2,128]{0,3,1,2:T(8,128)(2,1)S(1)}, u32[]{:S(2)}, u32[]{:S(2)}) collective-permute-start(bf16[256,4,2,128]{0,3,1,2:T(8,128)(2,1)S(1)} %collective-permute-done.4), channel_id=1, source_target_pairs={{0,2},{2,4},{4,6},{6,8},{8,10},{10,12},{12,14},{14,16},{16,18},{18... | collective-permute-start | bytes 1572872 | tf_op jit(solution)/shard_map/ppermute | solution.py:17
  127.4 7.7 %collective-permute-done.5 = bf16[256,4,2,128]{0,3,1,2:T(8,128)(2,1)S(1)} collective-permute-done((bf16[256,4,2,128]{0,3,1,2:T(8,128)(2,1)S(1)}, bf16[256,4,2,128]{0,3,1,2:T(8,128)(2,1)S(1)}, u32[]{:S(2)}, u32[]{:S(2)}) %collective-permute-start.5) | collective-permute-done | bytes 524320 | tf_op jit(solution)/shard_map/ppermute | solution.py:17
  135.9 6.1 %collective-permute-start.6 = (bf16[256,4,2,128]{0,3,1,2:T(8,128)(2,1)S(1)}, bf16[256,4,2,128]{0,3,1,2:T(8,128)(2,1)S(1)}, u32[]{:S(2)}, u32[]{:S(2)}) collective-permute-start(bf16[256,4,2,128]{0,3,1,2:T(8,128)(2,1)S(1)} %collective-permute-done.5), channel_id=1, source_target_pairs={{0,2},{2,4},{4,6},{6,8},{8,10},{10,12},{12,14},{14,16},{16,18},{18... | collective-permute-start | bytes 1572872 | tf_op jit(solution)/shard_map/ppermute | solution.py:17
  142.0 6.9 %collective-permute-done.6 = bf16[256,4,2,128]{0,3,1,2:T(8,128)(2,1)S(1)} collective-permute-done((bf16[256,4,2,128]{0,3,1,2:T(8,128)(2,1)S(1)}, bf16[256,4,2,128]{0,3,1,2:T(8,128)(2,1)S(1)}, u32[]{:S(2)}, u32[]{:S(2)}) %collective-permute-start.6) | collective-permute-done | bytes 524320 | tf_op jit(solution)/shard_map/ppermute | solution.py:17
  149.7 6.1 %collective-permute-start.7 = (bf16[256,4,2,128]{0,3,1,2:T(8,128)(2,1)S(1)}, bf16[256,4,2,128]{0,3,1,2:T(8,128)(2,1)S(1)}, u32[]{:S(2)}, u32[]{:S(2)}) collective-permute-start(bf16[256,4,2,128]{0,3,1,2:T(8,128)(2,1)S(1)} %collective-permute-done.6), channel_id=1, source_target_pairs={{0,2},{2,4},{4,6},{6,8},{8,10},{10,12},{12,14},{14,16},{16,18},{18... | collective-permute-start | bytes 1572872 | tf_op jit(solution)/shard_map/ppermute | solution.py:17
  155.8 6.7 %collective-permute-done.7 = bf16[256,4,2,128]{0,3,1,2:T(8,128)(2,1)S(1)} collective-permute-done((bf16[256,4,2,128]{0,3,1,2:T(8,128)(2,1)S(1)}, bf16[256,4,2,128]{0,3,1,2:T(8,128)(2,1)S(1)}, u32[]{:S(2)}, u32[]{:S(2)}) %collective-permute-start.7) | collective-permute-done | bytes 524320 | tf_op jit(solution)/shard_map/ppermute | solution.py:17
  163.3 6.1 %collective-permute-start.8 = (bf16[256,4,2,128]{0,3,1,2:T(8,128)(2,1)S(1)}, bf16[256,4,2,128]{0,3,1,2:T(8,128)(2,1)S(1)}, u32[]{:S(2)}, u32[]{:S(2)}) collective-permute-start(bf16[256,4,2,128]{0,3,1,2:T(8,128)(2,1)S(1)} %collective-permute-done.7), channel_id=1, source_target_pairs={{0,2},{2,4},{4,6},{6,8},{8,10},{10,12},{12,14},{14,16},{16,18},{18... | collective-permute-start | bytes 1572872 | tf_op jit(solution)/shard_map/ppermute | solution.py:17
  169.3 7.3 %collective-permute-done.8 = bf16[256,4,2,128]{0,3,1,2:T(8,128)(2,1)S(1)} collective-permute-done((bf16[256,4,2,128]{0,3,1,2:T(8,128)(2,1)S(1)}, bf16[256,4,2,128]{0,3,1,2:T(8,128)(2,1)S(1)}, u32[]{:S(2)}, u32[]{:S(2)}) %collective-permute-start.8) | collective-permute-done | bytes 524320 | tf_op jit(solution)/shard_map/ppermute | solution.py:17
  177.5 6.1 %collective-permute-start.9 = (bf16[256,4,2,128]{0,3,1,2:T(8,128)(2,1)S(1)}, bf16[256,4,2,128]{0,3,1,2:T(8,128)(2,1)S(1)}, u32[]{:S(2)}, u32[]{:S(2)}) collective-permute-start(bf16[256,4,2,128]{0,3,1,2:T(8,128)(2,1)S(1)} %collective-permute-done.8), channel_id=1, source_target_pairs={{0,2},{2,4},{4,6},{6,8},{8,10},{10,12},{12,14},{14,16},{16,18},{18... | collective-permute-start | bytes 1572872 | tf_op jit(solution)/shard_map/ppermute | solution.py:17
  183.6 8.5 %collective-permute-done.9 = bf16[256,4,2,128]{0,3,1,2:T(8,128)(2,1)S(1)} collective-permute-done((bf16[256,4,2,128]{0,3,1,2:T(8,128)(2,1)S(1)}, bf16[256,4,2,128]{0,3,1,2:T(8,128)(2,1)S(1)}, u32[]{:S(2)}, u32[]{:S(2)}) %collective-permute-start.9) | collective-permute-done | bytes 524320 | tf_op jit(solution)/shard_map/ppermute | solution.py:17
  192.9 6.1 %collective-permute-start.10 = (bf16[256,4,2,128]{0,3,1,2:T(8,128)(2,1)S(1)}, bf16[256,4,2,128]{0,3,1,2:T(8,128)(2,1)S(1)}, u32[]{:S(2)}, u32[]{:S(2)}) collective-permute-start(bf16[256,4,2,128]{0,3,1,2:T(8,128)(2,1)S(1)} %collective-permute-done.9), channel_id=1, source_target_pairs={{0,2},{2,4},{4,6},{6,8},{8,10},{10,12},{12,14},{14,16},{16,18},{18... | collective-permute-start | bytes 1572872 | tf_op jit(solution)/shard_map/ppermute | solution.py:17
  198.9 9.7 %collective-permute-done.10 = bf16[256,4,2,128]{0,3,1,2:T(8,128)(2,1)S(1)} collective-permute-done((bf16[256,4,2,128]{0,3,1,2:T(8,128)(2,1)S(1)}, bf16[256,4,2,128]{0,3,1,2:T(8,128)(2,1)S(1)}, u32[]{:S(2)}, u32[]{:S(2)}) %collective-permute-start.10) | collective-permute-done | bytes 524320 | tf_op jit(solution)/shard_map/ppermute | solution.py:17
  209.4 6.1 %collective-permute-start.11 = (bf16[256,4,2,128]{0,3,1,2:T(8,128)(2,1)S(1)}, bf16[256,4,2,128]{0,3,1,2:T(8,128)(2,1)}, u32[]{:S(2)}, u32[]{:S(2)}) collective-permute-start(bf16[256,4,2,128]{0,3,1,2:T(8,128)(2,1)S(1)} %collective-permute-done.10), channel_id=1, source_target_pairs={{0,2},{2,4},{4,6},{6,8},{8,10},{10,12},{12,14},{14,16},{16,18},{18... | collective-permute-start | bytes 1572872 | tf_op jit(solution)/shard_map/ppermute | solution.py:17
  215.5 11.3 %collective-permute-done.11 = bf16[256,4,2,128]{0,3,1,2:T(8,128)(2,1)} collective-permute-done((bf16[256,4,2,128]{0,3,1,2:T(8,128)(2,1)S(1)}, bf16[256,4,2,128]{0,3,1,2:T(8,128)(2,1)}, u32[]{:S(2)}, u32[]{:S(2)}) %collective-permute-start.11) | collective-permute-done | bytes 524320 | tf_op jit(solution)/shard_map/ppermute | solution.py:17
  226.7 6.2 %collective-permute-start.12 = (bf16[256,4,2,128]{0,3,1,2:T(8,128)(2,1)}, bf16[256,4,2,128]{0,3,1,2:T(8,128)(2,1)}, u32[]{:S(2)}, u32[]{:S(2)}) collective-permute-start(bf16[256,4,2,128]{0,3,1,2:T(8,128)(2,1)} %collective-permute-done.11), channel_id=1, source_target_pairs={{0,2},{2,4},{4,6},{6,8},{8,10},{10,12},{12,14},{14,16},{16,18},{18... | collective-permute-start | bytes 1572872 | tf_op jit(solution)/shard_map/ppermute | solution.py:17
  232.9 12.5 %collective-permute-done.12 = bf16[256,4,2,128]{0,3,1,2:T(8,128)(2,1)} collective-permute-done((bf16[256,4,2,128]{0,3,1,2:T(8,128)(2,1)}, bf16[256,4,2,128]{0,3,1,2:T(8,128)(2,1)}, u32[]{:S(2)}, u32[]{:S(2)}) %collective-permute-start.12) | collective-permute-done | bytes 524320 | tf_op jit(solution)/shard_map/ppermute | solution.py:17
  245.4 6.1 %collective-permute-start.13 = (bf16[256,4,2,128]{0,3,1,2:T(8,128)(2,1)}, bf16[256,4,2,128]{0,3,1,2:T(8,128)(2,1)}, u32[]{:S(2)}, u32[]{:S(2)}) collective-permute-start(bf16[256,4,2,128]{0,3,1,2:T(8,128)(2,1)} %collective-permute-done.12), channel_id=1, source_target_pairs={{0,2},{2,4},{4,6},{6,8},{8,10},{10,12},{12,14},{14,16},{16,18},{18... | collective-permute-start | bytes 1572872 | tf_op jit(solution)/shard_map/ppermute | solution.py:17
  263.2 6.1 %collective-permute-start.14 = (bf16[256,4,2,128]{0,3,1,2:T(8,128)(2,1)}, bf16[256,4,2,128]{0,3,1,2:T(8,128)(2,1)S(1)}, u32[]{:S(2)}, u32[]{:S(2)}) collective-permute-start(bf16[256,4,2,128]{0,3,1,2:T(8,128)(2,1)} %collective-permute-done.13), channel_id=1, source_target_pairs={{0,2},{2,4},{4,6},{6,8},{8,10},{10,12},{12,14},{14,16},{16,18},{18... | collective-permute-start | bytes 1572872 | tf_op jit(solution)/shard_map/ppermute | solution.py:17
  270.2 6.0 %collective-permute-done.14 = bf16[256,4,2,128]{0,3,1,2:T(8,128)(2,1)S(1)} collective-permute-done((bf16[256,4,2,128]{0,3,1,2:T(8,128)(2,1)}, bf16[256,4,2,128]{0,3,1,2:T(8,128)(2,1)S(1)}, u32[]{:S(2)}, u32[]{:S(2)}) %collective-permute-start.14) | collective-permute-done | bytes 524320 | tf_op jit(solution)/shard_map/ppermute | solution.py:17
  317.4 7.8 %constant_dynamic-slice_fusion.2 = bf16[4096,4,2,128]{0,3,1,2:T(8,128)(2,1)} fusion(bf16[8192,4,2,128]{0,3,1,2:T(8,128)(2,1)} %constant_dynamic-update-slice_fusion, s32[]{:T(128)S(6)} %select_n.57), kind=kLoop, calls=%fused_computation.94 | loop fusion | bytes 16777220 | tf_op jit(solution)/shard_map/jit(_roll_dynamic)/dynamic_slice | solution.py:20
  327.4 95.8 %while.20 = (s32[]{:T(128)}, f32[4,4,128]{2,1,0:T(4,128)S(1)}, f32[4,4,128]{2,1,0:T(4,128)S(1)}, f32[4,4,128,128]{3,2,1,0:T(8,128)}, f32[4,4,128]{2,1,0:T(4,128)...) while((s32[]{:T(128)}, f32[4,4,128]{2,1,0:T(4,128)S(1)}, ...), condition=%wide.region_14.15_spmd, body=%wide.region_4.14_spmd.sunk | while | flops 2203329536 | bytes 88360616 | solution.py:112
  334.1 8.8 %conditional.5 = ((f32[4,4,128]{2,1,0:T(4,128)S(1)}, f32[4,4,128]{2,1,0:T(4,128)S(1)}, f32[4,4,128,128]{3,2,1,0:T(8,128)})) conditional(s32[]{:T(128)} %convert_element_type.39, (f32[4,4,128]{2,1,0:T(4,128)S(1)}, f32[4,4,128]{2,1,0:T(4,128)S(1)}, f32[4,4,128,128]{3,2,1,0:T(8,128)}) %tuple.59, (s32[1024]{0:T(1024)S(1)}, s32[128]{0:T(128)S(1)}, ...), branch_computations={%region_10.10_spmd, %region_11.13_spmd} | conditional | flops 1101664256 | bytes 38933080 | solution.py:109
  338.9 2.9 fusion.21
  344.0 7.5 %conditional.4 = ((f32[4,4,128]{2,1,0:T(4,128)S(1)}, f32[4,4,128]{2,1,0:T(4,128)S(1)}, f32[4,4,128,128]{3,2,1,0:T(8,128)})) conditional(s32[]{:T(128)} %convert_element_type.38, (f32[4,4,128]{2,1,0:T(4,128)S(1)}, f32[4,4,128]{2,1,0:T(4,128)S(1)}, f32[4,4,128,128]{3,2,1,0:T(8,128)}) %tuple.57, (s32[1024]{0:T(1024)S(1)}, s32[128]{0:T(128)S(1)}, ...), branch_computations={%region_6.6_spmd, %region_7.9_spmd} | conditional | flops 1101664256 | bytes 38933080 | solution.py:109
  347.6 2.9 fusion.6
  358.0 8.8 %conditional.5 = ((f32[4,4,128]{2,1,0:T(4,128)S(1)}, f32[4,4,128]{2,1,0:T(4,128)S(1)}, f32[4,4,128,128]{3,2,1,0:T(8,128)})) conditional(s32[]{:T(128)} %convert_element_type.39, (f32[4,4,128]{2,1,0:T(4,128)S(1)}, f32[4,4,128]{2,1,0:T(4,128)S(1)}, f32[4,4,128,128]{3,2,1,0:T(8,128)}) %tuple.59, (s32[1024]{0:T(1024)S(1)}, s32[128]{0:T(128)S(1)}, ...), branch_computations={%region_10.10_spmd, %region_11.13_spmd} | conditional | flops 1101664256 | bytes 38933080 | solution.py:109
  362.8 2.9 fusion.21
  367.9 7.5 %conditional.4 = ((f32[4,4,128]{2,1,0:T(4,128)S(1)}, f32[4,4,128]{2,1,0:T(4,128)S(1)}, f32[4,4,128,128]{3,2,1,0:T(8,128)})) conditional(s32[]{:T(128)} %convert_element_type.38, (f32[4,4,128]{2,1,0:T(4,128)S(1)}, f32[4,4,128]{2,1,0:T(4,128)S(1)}, f32[4,4,128,128]{3,2,1,0:T(8,128)}) %tuple.57, (s32[1024]{0:T(1024)S(1)}, s32[128]{0:T(128)S(1)}, ...), branch_computations={%region_6.6_spmd, %region_7.9_spmd} | conditional | flops 1101664256 | bytes 38933080 | solution.py:109
  381.9 8.8 %conditional.5 = ((f32[4,4,128]{2,1,0:T(4,128)S(1)}, f32[4,4,128]{2,1,0:T(4,128)S(1)}, f32[4,4,128,128]{3,2,1,0:T(8,128)})) conditional(s32[]{:T(128)} %convert_element_type.39, (f32[4,4,128]{2,1,0:T(4,128)S(1)}, f32[4,4,128]{2,1,0:T(4,128)S(1)}, f32[4,4,128,128]{3,2,1,0:T(8,128)}) %tuple.59, (s32[1024]{0:T(1024)S(1)}, s32[128]{0:T(128)S(1)}, ...), branch_computations={%region_10.10_spmd, %region_11.13_spmd} | conditional | flops 1101664256 | bytes 38933080 | solution.py:109
  386.7 2.9 fusion.21
  391.8 7.5 %conditional.4 = ((f32[4,4,128]{2,1,0:T(4,128)S(1)}, f32[4,4,128]{2,1,0:T(4,128)S(1)}, f32[4,4,128,128]{3,2,1,0:T(8,128)})) conditional(s32[]{:T(128)} %convert_element_type.38, (f32[4,4,128]{2,1,0:T(4,128)S(1)}, f32[4,4,128]{2,1,0:T(4,128)S(1)}, f32[4,4,128,128]{3,2,1,0:T(8,128)}) %tuple.57, (s32[1024]{0:T(1024)S(1)}, s32[128]{0:T(128)S(1)}, ...), branch_computations={%region_6.6_spmd, %region_7.9_spmd} | conditional | flops 1101664256 | bytes 38933080 | solution.py:109
  405.8 8.8 %conditional.5 = ((f32[4,4,128]{2,1,0:T(4,128)S(1)}, f32[4,4,128]{2,1,0:T(4,128)S(1)}, f32[4,4,128,128]{3,2,1,0:T(8,128)})) conditional(s32[]{:T(128)} %convert_element_type.39, (f32[4,4,128]{2,1,0:T(4,128)S(1)}, f32[4,4,128]{2,1,0:T(4,128)S(1)}, f32[4,4,128,128]{3,2,1,0:T(8,128)}) %tuple.59, (s32[1024]{0:T(1024)S(1)}, s32[128]{0:T(128)S(1)}, ...), branch_computations={%region_10.10_spmd, %region_11.13_spmd} | conditional | flops 1101664256 | bytes 38933080 | solution.py:109
  410.6 2.9 fusion.21
  415.7 7.5 %conditional.4 = ((f32[4,4,128]{2,1,0:T(4,128)S(1)}, f32[4,4,128]{2,1,0:T(4,128)S(1)}, f32[4,4,128,128]{3,2,1,0:T(8,128)})) conditional(s32[]{:T(128)} %convert_element_type.38, (f32[4,4,128]{2,1,0:T(4,128)S(1)}, f32[4,4,128]{2,1,0:T(4,128)S(1)}, f32[4,4,128,128]{3,2,1,0:T(8,128)}) %tuple.57, (s32[1024]{0:T(1024)S(1)}, s32[128]{0:T(128)S(1)}, ...), branch_computations={%region_6.6_spmd, %region_7.9_spmd} | conditional | flops 1101664256 | bytes 38933080 | solution.py:109
  (205 shorter events, 134.6 us)
Async XLA Ops:
  0.0 22.7 %copy-start = (bf16[256,4096]{1,0:T(8,128)(2,1)S(1)}, bf16[256,4096]{1,0:T(8,128)(2,1)}, u32[]{:S(2)}) copy-start(bf16[256,4096]{1,0:T(8,128)(2,1)} %param.11) | copy-start | bytes 6291460
  22.7 20.7 %copy-start.22 = (u32[32]{0:T(128)S(1)}, u32[32]{0:T(128)}, u32[]{:S(2)}) copy-start(u32[32]{0:T(128)} %constant.102) | copy-start | bytes 388
  28.5 240.8 %copy-start.21 = (s32[32]{0:T(128)S(1)}, s32[32]{0:T(128)}, u32[]{:S(2)}) copy-start(s32[32]{0:T(128)} %param.15) | copy-start | bytes 388
  44.7 14.3 %collective-permute-start = (bf16[256,4,2,128]{0,3,1,2:T(8,128)(2,1)S(1)}, bf16[256,4,2,128]{0,3,1,2:T(8,128)(2,1)S(1)}, u32[]{:S(2)}, u32[]{:S(2)}) collective-permute-start(bf16[256,4,2,128]{0,3,1,2:T(8,128)(2,1)S(1)} %fusion.40), channel_id=1, source_target_pairs={{0,2},{2,4},{4,6},{6,8},{8,10},{10,12},{12,14},{14,16},{16,18},{18... | collective-permute-start | bytes 1572872 | tf_op jit(solution)/shard_map/ppermute | solution.py:17
  59.0 15.0 %collective-permute-start.1 = (bf16[256,4,2,128]{0,3,1,2:T(8,128)(2,1)S(1)}, bf16[256,4,2,128]{0,3,1,2:T(8,128)(2,1)S(1)}, u32[]{:S(2)}, u32[]{:S(2)}) collective-permute-start(bf16[256,4,2,128]{0,3,1,2:T(8,128)(2,1)S(1)} %collective-permute-done), channel_id=1, source_target_pairs={{0,2},{2,4},{4,6},{6,8},{8,10},{10,12},{12,14},{14,16},{16,18},{18... | collective-permute-start | bytes 1572872 | tf_op jit(solution)/shard_map/ppermute | solution.py:17
  74.0 16.4 %collective-permute-start.2 = (bf16[256,4,2,128]{0,3,1,2:T(8,128)(2,1)S(1)}, bf16[256,4,2,128]{0,3,1,2:T(8,128)(2,1)S(1)}, u32[]{:S(2)}, u32[]{:S(2)}) collective-permute-start(bf16[256,4,2,128]{0,3,1,2:T(8,128)(2,1)S(1)} %collective-permute-done.1), channel_id=1, source_target_pairs={{0,2},{2,4},{4,6},{6,8},{8,10},{10,12},{12,14},{14,16},{16,18},{18... | collective-permute-start | bytes 1572872 | tf_op jit(solution)/shard_map/ppermute | solution.py:17
  90.4 15.5 %collective-permute-start.3 = (bf16[256,4,2,128]{0,3,1,2:T(8,128)(2,1)S(1)}, bf16[256,4,2,128]{0,3,1,2:T(8,128)(2,1)S(1)}, u32[]{:S(2)}, u32[]{:S(2)}) collective-permute-start(bf16[256,4,2,128]{0,3,1,2:T(8,128)(2,1)S(1)} %collective-permute-done.2), channel_id=1, source_target_pairs={{0,2},{2,4},{4,6},{6,8},{8,10},{10,12},{12,14},{14,16},{16,18},{18... | collective-permute-start | bytes 1572872 | tf_op jit(solution)/shard_map/ppermute | solution.py:17
  105.9 14.6 %collective-permute-start.4 = (bf16[256,4,2,128]{0,3,1,2:T(8,128)(2,1)S(1)}, bf16[256,4,2,128]{0,3,1,2:T(8,128)(2,1)S(1)}, u32[]{:S(2)}, u32[]{:S(2)}) collective-permute-start(bf16[256,4,2,128]{0,3,1,2:T(8,128)(2,1)S(1)} %collective-permute-done.3), channel_id=1, source_target_pairs={{0,2},{2,4},{4,6},{6,8},{8,10},{10,12},{12,14},{14,16},{16,18},{18... | collective-permute-start | bytes 1572872 | tf_op jit(solution)/shard_map/ppermute | solution.py:17
  120.5 0.8 copy-start.7
  121.3 13.8 %collective-permute-start.5 = (bf16[256,4,2,128]{0,3,1,2:T(8,128)(2,1)S(1)}, bf16[256,4,2,128]{0,3,1,2:T(8,128)(2,1)S(1)}, u32[]{:S(2)}, u32[]{:S(2)}) collective-permute-start(bf16[256,4,2,128]{0,3,1,2:T(8,128)(2,1)S(1)} %collective-permute-done.4), channel_id=1, source_target_pairs={{0,2},{2,4},{4,6},{6,8},{8,10},{10,12},{12,14},{14,16},{16,18},{18... | collective-permute-start | bytes 1572872 | tf_op jit(solution)/shard_map/ppermute | solution.py:17
  135.1 0.8 copy-start.9
  135.9 12.9 %collective-permute-start.6 = (bf16[256,4,2,128]{0,3,1,2:T(8,128)(2,1)S(1)}, bf16[256,4,2,128]{0,3,1,2:T(8,128)(2,1)S(1)}, u32[]{:S(2)}, u32[]{:S(2)}) collective-permute-start(bf16[256,4,2,128]{0,3,1,2:T(8,128)(2,1)S(1)} %collective-permute-done.5), channel_id=1, source_target_pairs={{0,2},{2,4},{4,6},{6,8},{8,10},{10,12},{12,14},{14,16},{16,18},{18... | collective-permute-start | bytes 1572872 | tf_op jit(solution)/shard_map/ppermute | solution.py:17
  149.7 12.8 %collective-permute-start.7 = (bf16[256,4,2,128]{0,3,1,2:T(8,128)(2,1)S(1)}, bf16[256,4,2,128]{0,3,1,2:T(8,128)(2,1)S(1)}, u32[]{:S(2)}, u32[]{:S(2)}) collective-permute-start(bf16[256,4,2,128]{0,3,1,2:T(8,128)(2,1)S(1)} %collective-permute-done.6), channel_id=1, source_target_pairs={{0,2},{2,4},{4,6},{6,8},{8,10},{10,12},{12,14},{14,16},{16,18},{18... | collective-permute-start | bytes 1572872 | tf_op jit(solution)/shard_map/ppermute | solution.py:17
  163.3 13.4 %collective-permute-start.8 = (bf16[256,4,2,128]{0,3,1,2:T(8,128)(2,1)S(1)}, bf16[256,4,2,128]{0,3,1,2:T(8,128)(2,1)S(1)}, u32[]{:S(2)}, u32[]{:S(2)}) collective-permute-start(bf16[256,4,2,128]{0,3,1,2:T(8,128)(2,1)S(1)} %collective-permute-done.7), channel_id=1, source_target_pairs={{0,2},{2,4},{4,6},{6,8},{8,10},{10,12},{12,14},{14,16},{16,18},{18... | collective-permute-start | bytes 1572872 | tf_op jit(solution)/shard_map/ppermute | solution.py:17
  177.5 14.6 %collective-permute-start.9 = (bf16[256,4,2,128]{0,3,1,2:T(8,128)(2,1)S(1)}, bf16[256,4,2,128]{0,3,1,2:T(8,128)(2,1)S(1)}, u32[]{:S(2)}, u32[]{:S(2)}) collective-permute-start(bf16[256,4,2,128]{0,3,1,2:T(8,128)(2,1)S(1)} %collective-permute-done.8), channel_id=1, source_target_pairs={{0,2},{2,4},{4,6},{6,8},{8,10},{10,12},{12,14},{14,16},{16,18},{18... | collective-permute-start | bytes 1572872 | tf_op jit(solution)/shard_map/ppermute | solution.py:17
  192.9 15.7 %collective-permute-start.10 = (bf16[256,4,2,128]{0,3,1,2:T(8,128)(2,1)S(1)}, bf16[256,4,2,128]{0,3,1,2:T(8,128)(2,1)S(1)}, u32[]{:S(2)}, u32[]{:S(2)}) collective-permute-start(bf16[256,4,2,128]{0,3,1,2:T(8,128)(2,1)S(1)} %collective-permute-done.9), channel_id=1, source_target_pairs={{0,2},{2,4},{4,6},{6,8},{8,10},{10,12},{12,14},{14,16},{16,18},{18... | collective-permute-start | bytes 1572872 | tf_op jit(solution)/shard_map/ppermute | solution.py:17
  209.4 17.4 %collective-permute-start.11 = (bf16[256,4,2,128]{0,3,1,2:T(8,128)(2,1)S(1)}, bf16[256,4,2,128]{0,3,1,2:T(8,128)(2,1)}, u32[]{:S(2)}, u32[]{:S(2)}) collective-permute-start(bf16[256,4,2,128]{0,3,1,2:T(8,128)(2,1)S(1)} %collective-permute-done.10), channel_id=1, source_target_pairs={{0,2},{2,4},{4,6},{6,8},{8,10},{10,12},{12,14},{14,16},{16,18},{18... | collective-permute-start | bytes 1572872 | tf_op jit(solution)/shard_map/ppermute | solution.py:17
  226.7 18.7 %collective-permute-start.12 = (bf16[256,4,2,128]{0,3,1,2:T(8,128)(2,1)}, bf16[256,4,2,128]{0,3,1,2:T(8,128)(2,1)}, u32[]{:S(2)}, u32[]{:S(2)}) collective-permute-start(bf16[256,4,2,128]{0,3,1,2:T(8,128)(2,1)} %collective-permute-done.11), channel_id=1, source_target_pairs={{0,2},{2,4},{4,6},{6,8},{8,10},{10,12},{12,14},{14,16},{16,18},{18... | collective-permute-start | bytes 1572872 | tf_op jit(solution)/shard_map/ppermute | solution.py:17
  245.4 17.7 %collective-permute-start.13 = (bf16[256,4,2,128]{0,3,1,2:T(8,128)(2,1)}, bf16[256,4,2,128]{0,3,1,2:T(8,128)(2,1)}, u32[]{:S(2)}, u32[]{:S(2)}) collective-permute-start(bf16[256,4,2,128]{0,3,1,2:T(8,128)(2,1)} %collective-permute-done.12), channel_id=1, source_target_pairs={{0,2},{2,4},{4,6},{6,8},{8,10},{10,12},{12,14},{14,16},{16,18},{18... | collective-permute-start | bytes 1572872 | tf_op jit(solution)/shard_map/ppermute | solution.py:17
  262.1 44.9 %copy-start.20 = (bf16[256,4,2,128]{0,3,1,2:T(8,128)(2,1)S(1)}, bf16[256,4,2,128]{0,3,1,2:T(8,128)(2,1)}, u32[]{:S(2)}) copy-start(bf16[256,4,2,128]{0,3,1,2:T(8,128)(2,1)} %copy-done.19) | copy-start | bytes 1572868
  262.1 45.8 %copy-start.18 = (bf16[256,4,2,128]{0,3,1,2:T(8,128)(2,1)S(1)}, bf16[256,4,2,128]{0,3,1,2:T(8,128)(2,1)}, u32[]{:S(2)}) copy-start(bf16[256,4,2,128]{0,3,1,2:T(8,128)(2,1)} %copy-done.17) | copy-start | bytes 1572868
  262.1 46.7 %copy-start.16 = (bf16[256,4,2,128]{0,3,1,2:T(8,128)(2,1)S(1)}, bf16[256,4,2,128]{0,3,1,2:T(8,128)(2,1)}, u32[]{:S(2)}) copy-start(bf16[256,4,2,128]{0,3,1,2:T(8,128)(2,1)} %copy-done.15) | copy-start | bytes 1572868
  262.1 47.6 %copy-start.14 = (bf16[256,4,2,128]{0,3,1,2:T(8,128)(2,1)S(1)}, bf16[256,4,2,128]{0,3,1,2:T(8,128)(2,1)}, u32[]{:S(2)}) copy-start(bf16[256,4,2,128]{0,3,1,2:T(8,128)(2,1)} %copy-done.13) | copy-start | bytes 1572868
  262.1 48.5 %copy-start.12 = (bf16[256,4,2,128]{0,3,1,2:T(8,128)(2,1)S(1)}, bf16[256,4,2,128]{0,3,1,2:T(8,128)(2,1)}, u32[]{:S(2)}) copy-start(bf16[256,4,2,128]{0,3,1,2:T(8,128)(2,1)} %copy-done.11) | copy-start | bytes 1572868
  262.1 49.3 %copy-start.10 = (bf16[256,4,2,128]{0,3,1,2:T(8,128)(2,1)S(1)}, bf16[256,4,2,128]{0,3,1,2:T(8,128)(2,1)}, u32[]{:S(2)}) copy-start(bf16[256,4,2,128]{0,3,1,2:T(8,128)(2,1)} %copy-done.9) | copy-start | bytes 1572868
  262.1 50.2 %copy-start.8 = (bf16[256,4,2,128]{0,3,1,2:T(8,128)(2,1)S(1)}, bf16[256,4,2,128]{0,3,1,2:T(8,128)(2,1)}, u32[]{:S(2)}) copy-start(bf16[256,4,2,128]{0,3,1,2:T(8,128)(2,1)} %copy-done.7) | copy-start | bytes 1572868
  263.2 13.1 %collective-permute-start.14 = (bf16[256,4,2,128]{0,3,1,2:T(8,128)(2,1)}, bf16[256,4,2,128]{0,3,1,2:T(8,128)(2,1)S(1)}, u32[]{:S(2)}, u32[]{:S(2)}) collective-permute-start(bf16[256,4,2,128]{0,3,1,2:T(8,128)(2,1)} %collective-permute-done.13), channel_id=1, source_target_pairs={{0,2},{2,4},{4,6},{6,8},{8,10},{10,12},{12,14},{14,16},{16,18},{18... | collective-permute-start | bytes 1572872 | tf_op jit(solution)/shard_map/ppermute | solution.py:17
  334.1 10.0 %copy-start.2 = (bf16[128,4,4,128]{3,0,2,1:T(8,128)(2,1)S(1)}, bf16[128,4,4,128]{3,0,2,1:T(8,128)(2,1)}, u32[]{:S(2)}) copy-start(bf16[128,4,4,128]{3,0,2,1:T(8,128)(2,1)} %get-tuple-element.463) | copy-start | bytes 1572868 | tf_op jit(solution)/shard_map/while
  334.1 4.8 %copy-start.5 = (f32[4,4,128,128]{3,2,1,0:T(8,128)S(1)}, f32[4,4,128,128]{3,2,1,0:T(8,128)}, u32[]{:S(2)}) copy-start(f32[4,4,128,128]{3,2,1,0:T(8,128)} %get-tuple-element.127) | copy-start | bytes 3145732 | tf_op jit(solution)/shard_map/while/body/eval_jaxpr/cond
  341.8 1.0 copy-start.6
  344.0 3.6 copy-start.3
  350.6 1.0 copy-start.4
  358.0 10.0 %copy-start.2 = (bf16[128,4,4,128]{3,0,2,1:T(8,128)(2,1)S(1)}, bf16[128,4,4,128]{3,0,2,1:T(8,128)(2,1)}, u32[]{:S(2)}) copy-start(bf16[128,4,4,128]{3,0,2,1:T(8,128)(2,1)} %get-tuple-element.463) | copy-start | bytes 1572868 | tf_op jit(solution)/shard_map/while
  358.0 4.8 %copy-start.5 = (f32[4,4,128,128]{3,2,1,0:T(8,128)S(1)}, f32[4,4,128,128]{3,2,1,0:T(8,128)}, u32[]{:S(2)}) copy-start(f32[4,4,128,128]{3,2,1,0:T(8,128)} %get-tuple-element.127) | copy-start | bytes 3145732 | tf_op jit(solution)/shard_map/while/body/eval_jaxpr/cond
  365.7 1.0 copy-start.6
  367.9 3.6 copy-start.3
  374.5 1.0 copy-start.4
  381.9 10.0 %copy-start.2 = (bf16[128,4,4,128]{3,0,2,1:T(8,128)(2,1)S(1)}, bf16[128,4,4,128]{3,0,2,1:T(8,128)(2,1)}, u32[]{:S(2)}) copy-start(bf16[128,4,4,128]{3,0,2,1:T(8,128)(2,1)} %get-tuple-element.463) | copy-start | bytes 1572868 | tf_op jit(solution)/shard_map/while
  381.9 4.8 %copy-start.5 = (f32[4,4,128,128]{3,2,1,0:T(8,128)S(1)}, f32[4,4,128,128]{3,2,1,0:T(8,128)}, u32[]{:S(2)}) copy-start(f32[4,4,128,128]{3,2,1,0:T(8,128)} %get-tuple-element.127) | copy-start | bytes 3145732 | tf_op jit(solution)/shard_map/while/body/eval_jaxpr/cond
  389.6 1.0 copy-start.6
  391.9 3.6 copy-start.3
  398.4 1.0 copy-start.4
  405.8 10.0 %copy-start.2 = (bf16[128,4,4,128]{3,0,2,1:T(8,128)(2,1)S(1)}, bf16[128,4,4,128]{3,0,2,1:T(8,128)(2,1)}, u32[]{:S(2)}) copy-start(bf16[128,4,4,128]{3,0,2,1:T(8,128)(2,1)} %get-tuple-element.463) | copy-start | bytes 1572868 | tf_op jit(solution)/shard_map/while
  405.8 4.8 %copy-start.5 = (f32[4,4,128,128]{3,2,1,0:T(8,128)S(1)}, f32[4,4,128,128]{3,2,1,0:T(8,128)}, u32[]{:S(2)}) copy-start(f32[4,4,128,128]{3,2,1,0:T(8,128)} %get-tuple-element.127) | copy-start | bytes 3145732 | tf_op jit(solution)/shard_map/while/body/eval_jaxpr/cond
  413.5 1.0 copy-start.6
  415.8 3.6 copy-start.3
  422.3 1.0 copy-start.4
  423.3 4.6 %copy-start.1 = (bf16[256,4096]{1,0:T(8,128)(2,1)S(1)}, bf16[256,4096]{1,0:T(8,128)(2,1)}, u32[]{:S(2)}) copy-start(bf16[256,4096]{1,0:T(8,128)(2,1)} %param.11) | copy-start | bytes 6291460
  (5 other events, 4.0 us)
